TPU v7x, 16 devices: a 4x2x1 block of a 4x4x8 slice. The times are simulated.
16 devices in a mesh: dp: 2 (over y, z), cp: 8 (over x, core).
Axes of the slice: x: 4, y: 2, z: 1, core: 2. Of those that a mesh axis runs over, the one named last changes fastest.
The devices are a block of a 4x4x8 slice.
Arguments:
- hidden: bfloat16 [32, 2048, 5120], P('dp', 'cp'), parts along dimension 0
- positions: int32 [32, 2048], P('dp', 'cp'), parts along dimension 0
- w_q: bfloat16 [5120, 32, 128], replicated
- w_k: bfloat16 [5120, 8, 128], replicated
- w_v: bfloat16 [5120, 8, 128], replicated
- w_o: bfloat16 [32, 128, 5120], replicated
Outputs:
- output: bfloat16 [32, 2048, 5120], P('dp', 'cp'), parts along dimension 0
There are 2 independent parts. A program takes and returns all parts, laid end to end along the dimension named above; an argument that names none is the same for every part.
All inputs are finite; a program needn't handle non-finite values.
Results may differ from a plain program's by a relative error of at most 0.00862.
Values are sent between devices in bfloat16 or wider.
A program may use at most 768 MiB of HBM per device.

v0:
```python
import jax
import jax.numpy as jnp
from jax import lax
from jax.sharding import PartitionSpec as P

ROPE_BASE = 500000.0


def rope_tables(positions, head_dim):
    inv_freq = ROPE_BASE ** (-jnp.arange(0, head_dim, 2, dtype=jnp.float32) / head_dim)
    angles = positions.astype(jnp.float32)[..., None] * inv_freq
    angles = jnp.concatenate([angles, angles], axis=-1)
    return jnp.cos(angles)[:, :, None, :], jnp.sin(angles)[:, :, None, :]


def rope_apply(in_vals, cos_tab, sin_tab):
    half_dim = in_vals.shape[-1] // 2
    val_f32 = in_vals.astype(jnp.float32)
    rotated = jnp.concatenate([-val_f32[..., half_dim:], val_f32[..., :half_dim]], axis=-1)
    return (val_f32 * cos_tab + rotated * sin_tab).astype(jnp.bfloat16)


def project_qkv(hidden, positions, w_q, w_k, w_v):
    n_batch, tok_len = hidden.shape[0], hidden.shape[1]
    n_kv, head_dim = w_k.shape[1], w_k.shape[2]
    q_per_kv = w_q.shape[1] // n_kv
    queries = jnp.einsum('bsd,dhe->bshe', hidden, w_q, preferred_element_type=jnp.float32).astype(jnp.bfloat16)
    k_proj = jnp.einsum('bsd,dhe->bshe', hidden, w_k, preferred_element_type=jnp.float32).astype(jnp.bfloat16)
    values = jnp.einsum('bsd,dhe->bshe', hidden, w_v, preferred_element_type=jnp.float32).astype(jnp.bfloat16)
    cos_tab, sin_tab = rope_tables(positions, head_dim)
    queries = rope_apply(queries, cos_tab, sin_tab).reshape(n_batch, tok_len, n_kv, q_per_kv, head_dim)
    k_rot = rope_apply(k_proj, cos_tab, sin_tab)
    return queries, k_rot, values


def empty_state(queries):
    n_batch, tok_len, n_kv, q_per_kv, head_dim = queries.shape
    run_max = jnp.full((n_batch, n_kv, q_per_kv, tok_len), -jnp.inf, jnp.float32)
    run_sum = jnp.zeros((n_batch, n_kv, q_per_kv, tok_len), jnp.float32)
    out_acc = jnp.zeros((n_batch, n_kv, q_per_kv, tok_len, head_dim), jnp.float32)
    return run_max, run_sum, out_acc


def block_update(sm_state, queries, k_blk, v_blk, allowed):
    run_max, run_sum, out_acc = sm_state
    sm_scale = queries.shape[-1] ** -0.5
    scores = jnp.einsum('bqkge,bske->bkgqs', queries, k_blk, preferred_element_type=jnp.float32) * sm_scale
    scores = jnp.where(allowed, scores, -jnp.inf)
    new_max = jnp.maximum(run_max, jnp.max(scores, axis=-1))
    correction = jnp.exp(run_max - new_max)
    p_weights = jnp.exp(scores - new_max[..., None])
    run_sum = run_sum * correction + jnp.sum(p_weights, axis=-1)
    pv_part = jnp.einsum('bkgqs,bske->bkgqe', p_weights.astype(jnp.bfloat16), v_blk, preferred_element_type=jnp.float32)
    out_acc = out_acc * correction[..., None] + pv_part
    return new_max, run_sum, out_acc


def finish(sm_state, hidden, w_o):
    run_sum, out_acc = sm_state[1], sm_state[2]
    n_kv, q_per_kv, head_dim = out_acc.shape[1], out_acc.shape[2], out_acc.shape[4]
    attn_out = (out_acc / run_sum[..., None]).astype(jnp.bfloat16)
    w_o_grp = w_o.reshape(n_kv, q_per_kv, head_dim, w_o.shape[2])
    proj_out = jnp.einsum('clhrf,lhfe->cre', attn_out, w_o_grp, preferred_element_type=jnp.float32)
    return (hidden.astype(jnp.float32) + proj_out).astype(jnp.bfloat16)


def solution(mesh):
    cp_size = mesh.shape['cp']
    shift_pairs = [(j, (j + 1) % cp_size) for j in range(cp_size)]

    def per_device(hidden, positions, w_q, w_k, w_v, w_o):
        queries, k_rot, values = project_qkv(hidden, positions, w_q, w_k, w_v)
        tok_dev = hidden.shape[1]
        my_idx = lax.axis_index('cp')
        row_ids = jnp.arange(tok_dev)[:, None]
        col_ids = jnp.arange(tok_dev)[None, :]
        sm_state = block_update(empty_state(queries), queries, k_rot, values, col_ids <= row_ids)

        def kv_step(step_idx, loop_vals):
            cur_state, k_cur, v_cur = loop_vals
            k_cur = lax.ppermute(k_cur, 'cp', shift_pairs)
            v_cur = lax.ppermute(v_cur, 'cp', shift_pairs)
            src_idx = (my_idx - step_idx) % cp_size
            cur_state = block_update(cur_state, queries, k_cur, v_cur, src_idx < my_idx)
            return cur_state, k_cur, v_cur

        sm_state, k_last, v_last = lax.fori_loop(1, cp_size, kv_step, (sm_state, k_rot, values))
        return finish(sm_state, hidden, w_o)

    rep_spec = P(None, None, None)
    return jax.shard_map(per_device, mesh=mesh, in_specs=(P('dp', 'cp', None), P('dp', 'cp'), rep_spec, rep_spec, rep_spec, rep_spec), out_specs=P('dp', 'cp', None), check_vma=False)
```

profile of v0, /device:TPU:112, one launch (start us, length us, event | category | flops | bytes accessed | tf_op | source)
XLA Modules:
  0.0 3072.3 jit_solution(16187419603569083485)
XLA Ops:
  0.0 54.8 %copy.9 = bf16[5120,32,128]{0,2,1:T(8,128)(2,1)} copy(bf16[5120,32,128]{2,1,0:T(8,128)(2,1)} %param.10) | data formatting | bytes 83886080 | tf_op args[2]
  54.8 185.2 %convert_convert_fusion = f32[16,256,32,128]{1,3,2,0:T(8,128)} fusion(bf16[5120,32,128]{0,2,1:T(8,128)(2,1)} %copy.9, bf16[16,256,5120]{2,1,0:T(8,128)(2,1)} %param.8), kind=kOutput, calls=%fused_computation.45 | convolution fusion | flops 171832246272 | bytes 150994944 | tf_op jit(solution)/shard_map/bsd,dhe->bshe/dot_general | solution.py:27
  240.0 43.2 %slice_negate_fusion = (f32[16,256,32,64]{1,3,2,0:T(8,128)}, f32[16,256,32,64]{1,3,2,0:T(8,128)}) fusion(f32[16,256,32,128]{1,3,2,0:T(8,128)} %convert_convert_fusion), kind=kLoop, calls=%fused_computation.42 | loop fusion | flops 8388608 | bytes 134217728 | tf_op jit(solution)/shard_map/neg | solution.py:19
  290.7 53.6 %fusion.23 = bf16[16,256,32,128]{1,3,2,0:T(8,128)(2,1)} fusion(f32[16,256,32,64]{1,3,2,0:T(8,128)} %get-tuple-element.236, f32[16,256,32,64]{1,3,2,0:T(8,128)} %get-tuple-element.235, f32[16,256,32,128]{1,3,2,0:T(8,128)} %convert_convert_fusion, f32[16,256,128]{1,2,0:T(8,128)S(1)} %get-tuple-element.240, f32[16,256,128]{1,2,0:T(8,128)S(1)} %get-tuple-element.239), kind=kLoop, calls=%fused_computation.29 | loop fusion | flops 83886080 | bytes 171966464 | tf_op jit(solution)/shard_map/convert_element_type | solution.py:20
  344.3 14.4 copy.8
  358.7 53.1 %convert_convert_fusion.1 = f32[16,256,8,128]{1,3,2,0:T(8,128)} fusion(bf16[5120,8,128]{0,2,1:T(8,128)(2,1)} %copy.8, bf16[16,256,5120]{2,1,0:T(8,128)(2,1)} %param.8), kind=kOutput, calls=%fused_computation.56 | convolution fusion | flops 42958061568 | bytes 69206016 | tf_op jit(solution)/shard_map/bsd,dhe->bshe/dot_general | solution.py:28
  411.8 13.2 slice_negate_fusion.1
  428.2 10.6 fusion.43
  438.8 61.5 %fusion.18 = (f32[16,8,4,256]{3,2,1,0:T(4,128)}, f32[16,8,256,256,4]{3,2,4,1,0:T(8,128)}) fusion(pred[256,256]{0,1:T(8,128)(4,1)S(1)} %iota_compare_fusion, bf16[16,256,8,4,128]{1,4,3,2,0:T(8,128)(2,1)} %bitcast.135, bf16[16,256,8,128]{1,3,2,0:T(8,128)(2,1)} %fusion.43), kind=kOutput, calls=%fused_computation.23 | convolution fusion | flops 8690466816 | bytes 176750592 | tf_op jit(solution)/shard_map/bqkge,bske->bkgqs/dot_general | solution.py:47
  500.3 41.4 %fusion.17 = f32[16,8,4,256]{3,2,1,0:T(4,128)S(1)} fusion(f32[16,8,256,256,4]{3,2,4,1,0:T(8,128)} %get-tuple-element.244, f32[16,8,4,256]{3,2,1,0:T(4,128)} %get-tuple-element.307, pred[256,256]{0,1:T(8,128)(4,1)S(1)} %iota_compare_fusion), kind=kLoop, calls=%fused_computation.22 | loop fusion | flops 134086656 | bytes 135331840 | tf_op jit(solution)/shard_map/reduce_sum | solution.py:52
  543.9 50.2 %fusion.54 = bf16[16,256,8,128]{3,1,2,0:T(8,128)(2,1)S(1)} fusion(bf16[5120,8,128]{2,1,0:T(8,128)(2,1)} %param.12, bf16[16,256,5120]{2,1,0:T(8,128)(2,1)} %param.8), kind=kOutput, calls=%fused_computation.57 | convolution fusion | flops 42953867264 | bytes 60817408 | tf_op jit(solution)/shard_map/bsd,dhe->bshe/dot_general | solution.py:29
  594.1 81.2 %broadcast_add_fusion = f32[16,8,4,256,128]{4,3,2,1,0:T(8,128)} fusion(f32[16,8,4,256]{3,2,1,0:T(4,128)S(1)} %get-tuple-element.241, f32[16,8,256,256,4]{3,2,4,1,0:T(8,128)} %get-tuple-element.244, f32[16,8,4,256]{3,2,1,0:T(4,128)} %get-tuple-element.307, pred[256,256]{0,1:T(8,128)(4,1)S(1)} %iota_compare_fusion, bf16[16,256,8,128]{3,1,2,0:T(8,128)(2,1)S(1)} %fusion.54), kind=kOutput, calls=%fused_computation.44 | convolution fusion | flops 8740929536 | bytes 210829312 | tf_op jit(solution)/shard_map/bkgqs,bske->bkgqe/dot_general | solution.py:53
  675.3 42.0 %copy.15 = bf16[16,256,8,4,128]{4,1,3,2,0:T(8,128)(2,1)} copy(bf16[16,256,8,4,128]{1,4,3,2,0:T(8,128)(2,1)} %bitcast.136) | data formatting | bytes 67108864 | tf_op jit(solution)/shard_map/while | solution.py:87
  717.3 12.3 copy.14
  729.7 2117.4 %while.23 = (s32[]{:T(128)}, f32[16,8,4,256]{3,2,1,0:T(4,128)}, f32[16,8,4,256]{3,2,1,0:T(4,128)S(1)}, f32[16,8,4,256,128]{4,3,2,1,0:T(8,128)}, bf16[16,256,8,12...) while((s32[]{:T(128)}, f32[16,8,4,256]{3,2,1,0:T(4,128)}, ...), condition=%wide.region_5.6_spmd, body=%wide.region_2.5_spmd.sunk | while | flops 17582784512 | bytes 696254848 | solution.py:87
  732.1 92.1 %collective-permute-done = bf16[16,256,8,128]{3,1,2,0:T(8,128)(2,1)} collective-permute-done((bf16[16,256,8,128]{3,1,2,0:T(8,128)(2,1)}, bf16[16,256,8,128]{3,1,2,0:T(8,128)(2,1)}, u32[]{:S(2)}, u32[]{:S(2)}) %collective-permute-start) | collective-permute-done | bytes 8388640 | tf_op jit(solution)/shard_map/while/body/eval_jaxpr/ppermute | solution.py:81
  824.2 59.9 %bitcast_reduce_fusion.2 = (f32[16,8,4,256]{3,2,1,0:T(4,128)S(1)}, f32[16,8,256,256,4]{3,2,4,1,0:T(8,128)}) fusion(pred[]{:T(512)S(6)} %lt.31, bf16[16,256,8,4,128]{4,1,3,2,0:T(8,128)(2,1)} %get-tuple-element.337, bf16[16,256,8,128]{3,1,2,0:T(8,128)(2,1)} %collective-permute-done), kind=kOutput, calls=%fused_computation.1.clone.1 | convolution fusion | flops 8690466816 | bytes 176685056 | tf_op jit(solution)/shard_map/while/body/eval_jaxpr/bqkge,bske->bkgqs/dot_general | solution.py:47
  885.3 41.2 %fusion.81 = f32[16,8,4,256]{3,2,1,0:T(4,128)S(1)} fusion(f32[16,8,256,256,4]{3,2,4,1,0:T(8,128)} %get-tuple-element.303, f32[16,8,4,256]{3,2,1,0:T(4,128)S(1)} %max.11, pred[]{:T(512)S(6)} %lt.31), kind=kLoop, calls=%fused_computation.5.clone.1 | loop fusion | flops 134086656 | bytes 135266304 | tf_op jit(solution)/shard_map/while/body/eval_jaxpr/reduce_sum | solution.py:52
  936.6 7.8 copy.57
  944.4 88.1 %multiply_add_fusion.5 = f32[16,8,4,256,128]{4,3,2,1,0:T(8,128)} fusion(f32[16,8,4,256,128]{4,3,2,1,0:T(8,128)} %get-tuple-element.321, f32[16,8,4,256]{3,2,1,0:T(4,128)S(1)} %bitcast.137, f32[16,8,256,256,4]{3,2,4,1,0:T(8,128)} %get-tuple-element.303, f32[16,8,4,256]{3,2,1,0:T(4,128)S(1)} %max.11, pred[]{:T(512)S(6)} %lt.31, ...), kind=kOutput, calls=%fused_computation.7.clone.2 | convolution fusion | flops 8757706752 | bytes 277872640 | tf_op jit(solution)/shard_map/while/body/eval_jaxpr/bkgqs,bske->bkgqe/dot_general | solution.py:53
  1033.3 93.3 %collective-permute-done = bf16[16,256,8,128]{3,1,2,0:T(8,128)(2,1)} collective-permute-done((bf16[16,256,8,128]{3,1,2,0:T(8,128)(2,1)}, bf16[16,256,8,128]{3,1,2,0:T(8,128)(2,1)}, u32[]{:S(2)}, u32[]{:S(2)}) %collective-permute-start) | collective-permute-done | bytes 8388640 | tf_op jit(solution)/shard_map/while/body/eval_jaxpr/ppermute | solution.py:81
  1126.6 59.9 %bitcast_reduce_fusion.2 = (f32[16,8,4,256]{3,2,1,0:T(4,128)S(1)}, f32[16,8,256,256,4]{3,2,4,1,0:T(8,128)}) fusion(pred[]{:T(512)S(6)} %lt.31, bf16[16,256,8,4,128]{4,1,3,2,0:T(8,128)(2,1)} %get-tuple-element.337, bf16[16,256,8,128]{3,1,2,0:T(8,128)(2,1)} %collective-permute-done), kind=kOutput, calls=%fused_computation.1.clone.1 | convolution fusion | flops 8690466816 | bytes 176685056 | tf_op jit(solution)/shard_map/while/body/eval_jaxpr/bqkge,bske->bkgqs/dot_general | solution.py:47
  1187.7 41.2 %fusion.81 = f32[16,8,4,256]{3,2,1,0:T(4,128)S(1)} fusion(f32[16,8,256,256,4]{3,2,4,1,0:T(8,128)} %get-tuple-element.303, f32[16,8,4,256]{3,2,1,0:T(4,128)S(1)} %max.11, pred[]{:T(512)S(6)} %lt.31), kind=kLoop, calls=%fused_computation.5.clone.1 | loop fusion | flops 134086656 | bytes 135266304 | tf_op jit(solution)/shard_map/while/body/eval_jaxpr/reduce_sum | solution.py:52
  1239.1 7.8 copy.57
  1246.9 88.1 %multiply_add_fusion.5 = f32[16,8,4,256,128]{4,3,2,1,0:T(8,128)} fusion(f32[16,8,4,256,128]{4,3,2,1,0:T(8,128)} %get-tuple-element.321, f32[16,8,4,256]{3,2,1,0:T(4,128)S(1)} %bitcast.137, f32[16,8,256,256,4]{3,2,4,1,0:T(8,128)} %get-tuple-element.303, f32[16,8,4,256]{3,2,1,0:T(4,128)S(1)} %max.11, pred[]{:T(512)S(6)} %lt.31, ...), kind=kOutput, calls=%fused_computation.7.clone.2 | convolution fusion | flops 8757706752 | bytes 277872640 | tf_op jit(solution)/shard_map/while/body/eval_jaxpr/bkgqs,bske->bkgqe/dot_general | solution.py:53
  1335.0 94.1 %collective-permute-done = bf16[16,256,8,128]{3,1,2,0:T(8,128)(2,1)} collective-permute-done((bf16[16,256,8,128]{3,1,2,0:T(8,128)(2,1)}, bf16[16,256,8,128]{3,1,2,0:T(8,128)(2,1)}, u32[]{:S(2)}, u32[]{:S(2)}) %collective-permute-start) | collective-permute-done | bytes 8388640 | tf_op jit(solution)/shard_map/while/body/eval_jaxpr/ppermute | solution.py:81
  1429.0 59.9 %bitcast_reduce_fusion.2 = (f32[16,8,4,256]{3,2,1,0:T(4,128)S(1)}, f32[16,8,256,256,4]{3,2,4,1,0:T(8,128)}) fusion(pred[]{:T(512)S(6)} %lt.31, bf16[16,256,8,4,128]{4,1,3,2,0:T(8,128)(2,1)} %get-tuple-element.337, bf16[16,256,8,128]{3,1,2,0:T(8,128)(2,1)} %collective-permute-done), kind=kOutput, calls=%fused_computation.1.clone.1 | convolution fusion | flops 8690466816 | bytes 176685056 | tf_op jit(solution)/shard_map/while/body/eval_jaxpr/bqkge,bske->bkgqs/dot_general | solution.py:47
  1490.1 41.2 %fusion.81 = f32[16,8,4,256]{3,2,1,0:T(4,128)S(1)} fusion(f32[16,8,256,256,4]{3,2,4,1,0:T(8,128)} %get-tuple-element.303, f32[16,8,4,256]{3,2,1,0:T(4,128)S(1)} %max.11, pred[]{:T(512)S(6)} %lt.31), kind=kLoop, calls=%fused_computation.5.clone.1 | loop fusion | flops 134086656 | bytes 135266304 | tf_op jit(solution)/shard_map/while/body/eval_jaxpr/reduce_sum | solution.py:52
  1549.3 88.1 %multiply_add_fusion.5 = f32[16,8,4,256,128]{4,3,2,1,0:T(8,128)} fusion(f32[16,8,4,256,128]{4,3,2,1,0:T(8,128)} %get-tuple-element.321, f32[16,8,4,256]{3,2,1,0:T(4,128)S(1)} %bitcast.137, f32[16,8,256,256,4]{3,2,4,1,0:T(8,128)} %get-tuple-element.303, f32[16,8,4,256]{3,2,1,0:T(4,128)S(1)} %max.11, pred[]{:T(512)S(6)} %lt.31, ...), kind=kOutput, calls=%fused_computation.7.clone.2 | convolution fusion | flops 8757706752 | bytes 277872640 | tf_op jit(solution)/shard_map/while/body/eval_jaxpr/bkgqs,bske->bkgqe/dot_general | solution.py:53
  1637.4 94.1 %collective-permute-done = bf16[16,256,8,128]{3,1,2,0:T(8,128)(2,1)} collective-permute-done((bf16[16,256,8,128]{3,1,2,0:T(8,128)(2,1)}, bf16[16,256,8,128]{3,1,2,0:T(8,128)(2,1)}, u32[]{:S(2)}, u32[]{:S(2)}) %collective-permute-start) | collective-permute-done | bytes 8388640 | tf_op jit(solution)/shard_map/while/body/eval_jaxpr/ppermute | solution.py:81
  1731.4 59.9 %bitcast_reduce_fusion.2 = (f32[16,8,4,256]{3,2,1,0:T(4,128)S(1)}, f32[16,8,256,256,4]{3,2,4,1,0:T(8,128)}) fusion(pred[]{:T(512)S(6)} %lt.31, bf16[16,256,8,4,128]{4,1,3,2,0:T(8,128)(2,1)} %get-tuple-element.337, bf16[16,256,8,128]{3,1,2,0:T(8,128)(2,1)} %collective-permute-done), kind=kOutput, calls=%fused_computation.1.clone.1 | convolution fusion | flops 8690466816 | bytes 176685056 | tf_op jit(solution)/shard_map/while/body/eval_jaxpr/bqkge,bske->bkgqs/dot_general | solution.py:47
  1792.6 41.2 %fusion.81 = f32[16,8,4,256]{3,2,1,0:T(4,128)S(1)} fusion(f32[16,8,256,256,4]{3,2,4,1,0:T(8,128)} %get-tuple-element.303, f32[16,8,4,256]{3,2,1,0:T(4,128)S(1)} %max.11, pred[]{:T(512)S(6)} %lt.31), kind=kLoop, calls=%fused_computation.5.clone.1 | loop fusion | flops 134086656 | bytes 135266304 | tf_op jit(solution)/shard_map/while/body/eval_jaxpr/reduce_sum | solution.py:52
  1851.7 88.1 %multiply_add_fusion.5 = f32[16,8,4,256,128]{4,3,2,1,0:T(8,128)} fusion(f32[16,8,4,256,128]{4,3,2,1,0:T(8,128)} %get-tuple-element.321, f32[16,8,4,256]{3,2,1,0:T(4,128)S(1)} %bitcast.137, f32[16,8,256,256,4]{3,2,4,1,0:T(8,128)} %get-tuple-element.303, f32[16,8,4,256]{3,2,1,0:T(4,128)S(1)} %max.11, pred[]{:T(512)S(6)} %lt.31, ...), kind=kOutput, calls=%fused_computation.7.clone.2 | convolution fusion | flops 8757706752 | bytes 277872640 | tf_op jit(solution)/shard_map/while/body/eval_jaxpr/bkgqs,bske->bkgqe/dot_general | solution.py:53
  1939.8 94.1 %collective-permute-done = bf16[16,256,8,128]{3,1,2,0:T(8,128)(2,1)} collective-permute-done((bf16[16,256,8,128]{3,1,2,0:T(8,128)(2,1)}, bf16[16,256,8,128]{3,1,2,0:T(8,128)(2,1)}, u32[]{:S(2)}, u32[]{:S(2)}) %collective-permute-start) | collective-permute-done | bytes 8388640 | tf_op jit(solution)/shard_map/while/body/eval_jaxpr/ppermute | solution.py:81
  2033.9 59.9 %bitcast_reduce_fusion.2 = (f32[16,8,4,256]{3,2,1,0:T(4,128)S(1)}, f32[16,8,256,256,4]{3,2,4,1,0:T(8,128)}) fusion(pred[]{:T(512)S(6)} %lt.31, bf16[16,256,8,4,128]{4,1,3,2,0:T(8,128)(2,1)} %get-tuple-element.337, bf16[16,256,8,128]{3,1,2,0:T(8,128)(2,1)} %collective-permute-done), kind=kOutput, calls=%fused_computation.1.clone.1 | convolution fusion | flops 8690466816 | bytes 176685056 | tf_op jit(solution)/shard_map/while/body/eval_jaxpr/bqkge,bske->bkgqs/dot_general | solution.py:47
  2095.0 41.2 %fusion.81 = f32[16,8,4,256]{3,2,1,0:T(4,128)S(1)} fusion(f32[16,8,256,256,4]{3,2,4,1,0:T(8,128)} %get-tuple-element.303, f32[16,8,4,256]{3,2,1,0:T(4,128)S(1)} %max.11, pred[]{:T(512)S(6)} %lt.31), kind=kLoop, calls=%fused_computation.5.clone.1 | loop fusion | flops 134086656 | bytes 135266304 | tf_op jit(solution)/shard_map/while/body/eval_jaxpr/reduce_sum | solution.py:52
  2154.1 88.1 %multiply_add_fusion.5 = f32[16,8,4,256,128]{4,3,2,1,0:T(8,128)} fusion(f32[16,8,4,256,128]{4,3,2,1,0:T(8,128)} %get-tuple-element.321, f32[16,8,4,256]{3,2,1,0:T(4,128)S(1)} %bitcast.137, f32[16,8,256,256,4]{3,2,4,1,0:T(8,128)} %get-tuple-element.303, f32[16,8,4,256]{3,2,1,0:T(4,128)S(1)} %max.11, pred[]{:T(512)S(6)} %lt.31, ...), kind=kOutput, calls=%fused_computation.7.clone.2 | convolution fusion | flops 8757706752 | bytes 277872640 | tf_op jit(solution)/shard_map/while/body/eval_jaxpr/bkgqs,bske->bkgqe/dot_general | solution.py:53
  2242.2 94.1 %collective-permute-done = bf16[16,256,8,128]{3,1,2,0:T(8,128)(2,1)} collective-permute-done((bf16[16,256,8,128]{3,1,2,0:T(8,128)(2,1)}, bf16[16,256,8,128]{3,1,2,0:T(8,128)(2,1)}, u32[]{:S(2)}, u32[]{:S(2)}) %collective-permute-start) | collective-permute-done | bytes 8388640 | tf_op jit(solution)/shard_map/while/body/eval_jaxpr/ppermute | solution.py:81
  2336.3 59.9 %bitcast_reduce_fusion.2 = (f32[16,8,4,256]{3,2,1,0:T(4,128)S(1)}, f32[16,8,256,256,4]{3,2,4,1,0:T(8,128)}) fusion(pred[]{:T(512)S(6)} %lt.31, bf16[16,256,8,4,128]{4,1,3,2,0:T(8,128)(2,1)} %get-tuple-element.337, bf16[16,256,8,128]{3,1,2,0:T(8,128)(2,1)} %collective-permute-done), kind=kOutput, calls=%fused_computation.1.clone.1 | convolution fusion | flops 8690466816 | bytes 176685056 | tf_op jit(solution)/shard_map/while/body/eval_jaxpr/bqkge,bske->bkgqs/dot_general | solution.py:47
  2397.4 41.2 %fusion.81 = f32[16,8,4,256]{3,2,1,0:T(4,128)S(1)} fusion(f32[16,8,256,256,4]{3,2,4,1,0:T(8,128)} %get-tuple-element.303, f32[16,8,4,256]{3,2,1,0:T(4,128)S(1)} %max.11, pred[]{:T(512)S(6)} %lt.31), kind=kLoop, calls=%fused_computation.5.clone.1 | loop fusion | flops 134086656 | bytes 135266304 | tf_op jit(solution)/shard_map/while/body/eval_jaxpr/reduce_sum | solution.py:52
  2448.8 7.8 copy.57
  2456.6 88.1 %multiply_add_fusion.5 = f32[16,8,4,256,128]{4,3,2,1,0:T(8,128)} fusion(f32[16,8,4,256,128]{4,3,2,1,0:T(8,128)} %get-tuple-element.321, f32[16,8,4,256]{3,2,1,0:T(4,128)S(1)} %bitcast.137, f32[16,8,256,256,4]{3,2,4,1,0:T(8,128)} %get-tuple-element.303, f32[16,8,4,256]{3,2,1,0:T(4,128)S(1)} %max.11, pred[]{:T(512)S(6)} %lt.31, ...), kind=kOutput, calls=%fused_computation.7.clone.2 | convolution fusion | flops 8757706752 | bytes 277872640 | tf_op jit(solution)/shard_map/while/body/eval_jaxpr/bkgqs,bske->bkgqe/dot_general | solution.py:53
  2544.7 94.1 %collective-permute-done = bf16[16,256,8,128]{3,1,2,0:T(8,128)(2,1)} collective-permute-done((bf16[16,256,8,128]{3,1,2,0:T(8,128)(2,1)}, bf16[16,256,8,128]{3,1,2,0:T(8,128)(2,1)}, u32[]{:S(2)}, u32[]{:S(2)}) %collective-permute-start) | collective-permute-done | bytes 8388640 | tf_op jit(solution)/shard_map/while/body/eval_jaxpr/ppermute | solution.py:81
  2638.7 59.9 %bitcast_reduce_fusion.2 = (f32[16,8,4,256]{3,2,1,0:T(4,128)S(1)}, f32[16,8,256,256,4]{3,2,4,1,0:T(8,128)}) fusion(pred[]{:T(512)S(6)} %lt.31, bf16[16,256,8,4,128]{4,1,3,2,0:T(8,128)(2,1)} %get-tuple-element.337, bf16[16,256,8,128]{3,1,2,0:T(8,128)(2,1)} %collective-permute-done), kind=kOutput, calls=%fused_computation.1.clone.1 | convolution fusion | flops 8690466816 | bytes 176685056 | tf_op jit(solution)/shard_map/while/body/eval_jaxpr/bqkge,bske->bkgqs/dot_general | solution.py:47
  2699.8 41.2 %fusion.81 = f32[16,8,4,256]{3,2,1,0:T(4,128)S(1)} fusion(f32[16,8,256,256,4]{3,2,4,1,0:T(8,128)} %get-tuple-element.303, f32[16,8,4,256]{3,2,1,0:T(4,128)S(1)} %max.11, pred[]{:T(512)S(6)} %lt.31), kind=kLoop, calls=%fused_computation.5.clone.1 | loop fusion | flops 134086656 | bytes 135266304 | tf_op jit(solution)/shard_map/while/body/eval_jaxpr/reduce_sum | solution.py:52
  2751.2 7.8 copy.57
  2759.0 88.1 %multiply_add_fusion.5 = f32[16,8,4,256,128]{4,3,2,1,0:T(8,128)} fusion(f32[16,8,4,256,128]{4,3,2,1,0:T(8,128)} %get-tuple-element.321, f32[16,8,4,256]{3,2,1,0:T(4,128)S(1)} %bitcast.137, f32[16,8,256,256,4]{3,2,4,1,0:T(8,128)} %get-tuple-element.303, f32[16,8,4,256]{3,2,1,0:T(4,128)S(1)} %max.11, pred[]{:T(512)S(6)} %lt.31, ...), kind=kOutput, calls=%fused_computation.7.clone.2 | convolution fusion | flops 8757706752 | bytes 277872640 | tf_op jit(solution)/shard_map/while/body/eval_jaxpr/bkgqs,bske->bkgqe/dot_general | solution.py:53
  2847.1 224.8 %fusion.19 = bf16[16,256,5120]{2,1,0:T(8,128)(2,1)} fusion(bf16[16,256,5120]{2,1,0:T(8,128)(2,1)} %param.8, bf16[8,4,128,5120,1]{3,2,1,0,4:T(8,128)(2,1)} %bitcast.141, f32[16,8,4,256,128]{4,3,2,1,0:T(8,128)} %get-tuple-element.205, f32[16,8,4,256]{3,2,1,0:T(4,128)S(1)} %get-tuple-element.206), kind=kOutput, calls=%fused_computation.25 | convolution fusion | flops 171895160832 | bytes 193462272 | tf_op jit(solution)/shard_map/clhrf,lhfe->cre/dot_general | solution.py:63
  (70 shorter events, 118.4 us)
Async XLA Ops:
  240.0 43.2 %copy-start.4 = (s32[16,256]{1,0:T(8,128)S(1)}, s32[16,256]{1,0:T(8,128)}, u32[]{:S(2)}) copy-start(s32[16,256]{1,0:T(8,128)} %param.9) | copy-start | bytes 49156
  290.6 53.7 %copy-start.1 = (f32[16,256,128]{1,2,0:T(8,128)}, f32[16,256,128]{1,2,0:T(8,128)S(1)}, u32[]{:S(2)}) copy-start(f32[16,256,128]{1,2,0:T(8,128)S(1)} %get-tuple-element.240) | copy-start | bytes 6291460
  358.7 66.4 %copy-start.2 = (f32[16,256,128]{1,2,0:T(8,128)S(1)}, f32[16,256,128]{1,2,0:T(8,128)}, u32[]{:S(2)}) copy-start(f32[16,256,128]{1,2,0:T(8,128)} %copy-done.1) | copy-start | bytes 6291460
  411.8 16.3 copy-start
  594.1 81.2 %copy-start.5 = (bf16[16,256,8,128]{3,1,2,0:T(8,128)(2,1)}, bf16[16,256,8,128]{3,1,2,0:T(8,128)(2,1)S(1)}, u32[]{:S(2)}) copy-start(bf16[16,256,8,128]{3,1,2,0:T(8,128)(2,1)S(1)} %fusion.54) | copy-start | bytes 25165828
  675.3 54.4 %copy-start.3 = (f32[16,8,4,256]{3,2,1,0:T(4,128)S(1)}, f32[16,8,4,256]{3,2,1,0:T(4,128)}, u32[]{:S(2)}) copy-start(f32[16,8,4,256]{3,2,1,0:T(4,128)} %get-tuple-element.308) | copy-start | bytes 1572868
  729.7 94.5 %collective-permute-start = (bf16[16,256,8,128]{3,1,2,0:T(8,128)(2,1)}, bf16[16,256,8,128]{3,1,2,0:T(8,128)(2,1)}, u32[]{:S(2)}, u32[]{:S(2)}) collective-permute-start(bf16[16,256,8,128]{3,1,2,0:T(8,128)(2,1)} %get-tuple-element.322), channel_id=1, source_target_pairs={{0,1},{1,2},{2,3},{3,4},{4,5},{5,6},{6,7},{7,0},{8,9},{9,10},{10,1... | collective-permute-start | bytes 25165832 | tf_op jit(solution)/shard_map/while/body/eval_jaxpr/ppermute | solution.py:81
  729.7 207.0 %collective-permute-start.1 = (bf16[16,256,8,128]{3,1,2,0:T(8,128)(2,1)}, bf16[16,256,8,128]{3,1,2,0:T(8,128)(2,1)}, u32[]{:S(2)}, u32[]{:S(2)}) collective-permute-start(bf16[16,256,8,128]{3,1,2,0:T(8,128)(2,1)} %get-tuple-element.323), channel_id=1, source_target_pairs={{0,1},{1,2},{2,3},{3,4},{4,5},{5,6},{6,7},{7,0},{8,9},{9,10},{10,1... | collective-permute-start | bytes 25165832 | tf_op jit(solution)/shard_map/while/body/eval_jaxpr/ppermute | solution.py:82
  1032.5 94.1 %collective-permute-start = (bf16[16,256,8,128]{3,1,2,0:T(8,128)(2,1)}, bf16[16,256,8,128]{3,1,2,0:T(8,128)(2,1)}, u32[]{:S(2)}, u32[]{:S(2)}) collective-permute-start(bf16[16,256,8,128]{3,1,2,0:T(8,128)(2,1)} %get-tuple-element.322), channel_id=1, source_target_pairs={{0,1},{1,2},{2,3},{3,4},{4,5},{5,6},{6,7},{7,0},{8,9},{9,10},{10,1... | collective-permute-start | bytes 25165832 | tf_op jit(solution)/shard_map/while/body/eval_jaxpr/ppermute | solution.py:81
  1032.5 206.5 %collective-permute-start.1 = (bf16[16,256,8,128]{3,1,2,0:T(8,128)(2,1)}, bf16[16,256,8,128]{3,1,2,0:T(8,128)(2,1)}, u32[]{:S(2)}, u32[]{:S(2)}) collective-permute-start(bf16[16,256,8,128]{3,1,2,0:T(8,128)(2,1)} %get-tuple-element.323), channel_id=1, source_target_pairs={{0,1},{1,2},{2,3},{3,4},{4,5},{5,6},{6,7},{7,0},{8,9},{9,10},{10,1... | collective-permute-start | bytes 25165832 | tf_op jit(solution)/shard_map/while/body/eval_jaxpr/ppermute | solution.py:82
  1334.9 94.1 %collective-permute-start = (bf16[16,256,8,128]{3,1,2,0:T(8,128)(2,1)}, bf16[16,256,8,128]{3,1,2,0:T(8,128)(2,1)}, u32[]{:S(2)}, u32[]{:S(2)}) collective-permute-start(bf16[16,256,8,128]{3,1,2,0:T(8,128)(2,1)} %get-tuple-element.322), channel_id=1, source_target_pairs={{0,1},{1,2},{2,3},{3,4},{4,5},{5,6},{6,7},{7,0},{8,9},{9,10},{10,1... | collective-permute-start | bytes 25165832 | tf_op jit(solution)/shard_map/while/body/eval_jaxpr/ppermute | solution.py:81
  1334.9 206.5 %collective-permute-start.1 = (bf16[16,256,8,128]{3,1,2,0:T(8,128)(2,1)}, bf16[16,256,8,128]{3,1,2,0:T(8,128)(2,1)}, u32[]{:S(2)}, u32[]{:S(2)}) collective-permute-start(bf16[16,256,8,128]{3,1,2,0:T(8,128)(2,1)} %get-tuple-element.323), channel_id=1, source_target_pairs={{0,1},{1,2},{2,3},{3,4},{4,5},{5,6},{6,7},{7,0},{8,9},{9,10},{10,1... | collective-permute-start | bytes 25165832 | tf_op jit(solution)/shard_map/while/body/eval_jaxpr/ppermute | solution.py:82
  1637.4 94.1 %collective-permute-start = (bf16[16,256,8,128]{3,1,2,0:T(8,128)(2,1)}, bf16[16,256,8,128]{3,1,2,0:T(8,128)(2,1)}, u32[]{:S(2)}, u32[]{:S(2)}) collective-permute-start(bf16[16,256,8,128]{3,1,2,0:T(8,128)(2,1)} %get-tuple-element.322), channel_id=1, source_target_pairs={{0,1},{1,2},{2,3},{3,4},{4,5},{5,6},{6,7},{7,0},{8,9},{9,10},{10,1... | collective-permute-start | bytes 25165832 | tf_op jit(solution)/shard_map/while/body/eval_jaxpr/ppermute | solution.py:81
  1637.4 206.5 %collective-permute-start.1 = (bf16[16,256,8,128]{3,1,2,0:T(8,128)(2,1)}, bf16[16,256,8,128]{3,1,2,0:T(8,128)(2,1)}, u32[]{:S(2)}, u32[]{:S(2)}) collective-permute-start(bf16[16,256,8,128]{3,1,2,0:T(8,128)(2,1)} %get-tuple-element.323), channel_id=1, source_target_pairs={{0,1},{1,2},{2,3},{3,4},{4,5},{5,6},{6,7},{7,0},{8,9},{9,10},{10,1... | collective-permute-start | bytes 25165832 | tf_op jit(solution)/shard_map/while/body/eval_jaxpr/ppermute | solution.py:82
  1939.8 94.1 %collective-permute-start = (bf16[16,256,8,128]{3,1,2,0:T(8,128)(2,1)}, bf16[16,256,8,128]{3,1,2,0:T(8,128)(2,1)}, u32[]{:S(2)}, u32[]{:S(2)}) collective-permute-start(bf16[16,256,8,128]{3,1,2,0:T(8,128)(2,1)} %get-tuple-element.322), channel_id=1, source_target_pairs={{0,1},{1,2},{2,3},{3,4},{4,5},{5,6},{6,7},{7,0},{8,9},{9,10},{10,1... | collective-permute-start | bytes 25165832 | tf_op jit(solution)/shard_map/while/body/eval_jaxpr/ppermute | solution.py:81
  1939.8 206.5 %collective-permute-start.1 = (bf16[16,256,8,128]{3,1,2,0:T(8,128)(2,1)}, bf16[16,256,8,128]{3,1,2,0:T(8,128)(2,1)}, u32[]{:S(2)}, u32[]{:S(2)}) collective-permute-start(bf16[16,256,8,128]{3,1,2,0:T(8,128)(2,1)} %get-tuple-element.323), channel_id=1, source_target_pairs={{0,1},{1,2},{2,3},{3,4},{4,5},{5,6},{6,7},{7,0},{8,9},{9,10},{10,1... | collective-permute-start | bytes 25165832 | tf_op jit(solution)/shard_map/while/body/eval_jaxpr/ppermute | solution.py:82
  2242.2 94.1 %collective-permute-start = (bf16[16,256,8,128]{3,1,2,0:T(8,128)(2,1)}, bf16[16,256,8,128]{3,1,2,0:T(8,128)(2,1)}, u32[]{:S(2)}, u32[]{:S(2)}) collective-permute-start(bf16[16,256,8,128]{3,1,2,0:T(8,128)(2,1)} %get-tuple-element.322), channel_id=1, source_target_pairs={{0,1},{1,2},{2,3},{3,4},{4,5},{5,6},{6,7},{7,0},{8,9},{9,10},{10,1... | collective-permute-start | bytes 25165832 | tf_op jit(solution)/shard_map/while/body/eval_jaxpr/ppermute | solution.py:81
  2242.2 206.5 %collective-permute-start.1 = (bf16[16,256,8,128]{3,1,2,0:T(8,128)(2,1)}, bf16[16,256,8,128]{3,1,2,0:T(8,128)(2,1)}, u32[]{:S(2)}, u32[]{:S(2)}) collective-permute-start(bf16[16,256,8,128]{3,1,2,0:T(8,128)(2,1)} %get-tuple-element.323), channel_id=1, source_target_pairs={{0,1},{1,2},{2,3},{3,4},{4,5},{5,6},{6,7},{7,0},{8,9},{9,10},{10,1... | collective-permute-start | bytes 25165832 | tf_op jit(solution)/shard_map/while/body/eval_jaxpr/ppermute | solution.py:82
  2544.6 94.1 %collective-permute-start = (bf16[16,256,8,128]{3,1,2,0:T(8,128)(2,1)}, bf16[16,256,8,128]{3,1,2,0:T(8,128)(2,1)}, u32[]{:S(2)}, u32[]{:S(2)}) collective-permute-start(bf16[16,256,8,128]{3,1,2,0:T(8,128)(2,1)} %get-tuple-element.322), channel_id=1, source_target_pairs={{0,1},{1,2},{2,3},{3,4},{4,5},{5,6},{6,7},{7,0},{8,9},{9,10},{10,1... | collective-permute-start | bytes 25165832 | tf_op jit(solution)/shard_map/while/body/eval_jaxpr/ppermute | solution.py:81
  2544.6 206.5 %collective-permute-start.1 = (bf16[16,256,8,128]{3,1,2,0:T(8,128)(2,1)}, bf16[16,256,8,128]{3,1,2,0:T(8,128)(2,1)}, u32[]{:S(2)}, u32[]{:S(2)}) collective-permute-start(bf16[16,256,8,128]{3,1,2,0:T(8,128)(2,1)} %get-tuple-element.323), channel_id=1, source_target_pairs={{0,1},{1,2},{2,3},{3,4},{4,5},{5,6},{6,7},{7,0},{8,9},{9,10},{10,1... | collective-permute-start | bytes 25165832 | tf_op jit(solution)/shard_map/while/body/eval_jaxpr/ppermute | solution.py:82
where the time goes:
time: 3090 us; the launch traced here: 3070 us
  matrix products  1690 us (55%)
  waiting for transfers between devices  656 us (21%)
  other arithmetic  479 us (16%)
  local copies, waits for them, and re-layouts  241 us (8%)
    dot_general x8, matrix products, block_update(): jnp.einsum('bkgqs,bske->bkgqe', p_weights.astype(jnp.bfloat16), v_blk, pr...  698 us
    ppermute x7, waiting for transfers between devices, kv_step(): k_cur = lax.ppermute(k_cur, 'cp', shift_pairs)  656 us
    dot_general x8, matrix products, block_update(): jnp.einsum('bqkge,bske->bkgqs', queries, k_blk, preferred_element_type=jn...  481 us
    reduce_sum x8, other arithmetic, block_update(): run_sum = run_sum * correction + jnp.sum(p_weights, axis=-1)  330 us
    dot_general x1, matrix products, finish(): jnp.einsum('clhrf,lhfe->cre', attn_out, w_o_grp, preferred_element_type=j...  225 us
    dot_general x1, matrix products, project_qkv(): jnp.einsum('bsd,dhe->bshe', hidden, w_q, preferred_element_type=jnp.float32)  185 us
    while x21, local copies, waits for them, and re-layouts  115 us
    unnamed x14, local copies, waits for them, and re-layouts  72.3 us
  transfers between devices with their start and end apart: 14, of which 7 were waited for; matrix products, arithmetic and copies ran while one was open for 26% of the time, Pallas kernels for 0%

commit v1 on v0

v1 whole, which is shorter than its diff:
```python
import functools

import jax
import jax.numpy as jnp
from jax import lax
from jax.experimental import pallas as pl
from jax.experimental.pallas import tpu as pltpu
from jax.experimental.layout import Layout, with_layout_constraint
from jax.sharding import PartitionSpec as P

ROPE_BASE = 500000.0
LOG2E = 1.4426950408889634
N_CHUNKS = 2


def VARIANTS(n_dev):
    return sorted({max(n_dev // 2 - 1, 1), max(n_dev - 1, 1), n_dev})


def rope_tables(positions, head_dim):
    half = head_dim // 2
    inv_freq = ROPE_BASE ** (-jnp.arange(0, head_dim, 2, dtype=jnp.float32) / head_dim)
    angles = positions.astype(jnp.float32)[..., None] * inv_freq
    angles = jnp.concatenate([angles, angles], axis=-1)
    sign = jnp.where(jnp.arange(head_dim) < half, -1.0, 1.0).astype(jnp.float32)
    return jnp.cos(angles), jnp.sin(angles) * sign


def rope_block(val, cos_tab, sin_tab):
    v = val.astype(jnp.float32)
    return (v * cos_tab + pltpu.roll(v, v.shape[-1] // 2, v.ndim - 1) * sin_tab).astype(jnp.bfloat16)


def k_rope_kernel(k_ref, cos_ref, sin_ref, o_ref):
    cos_tab, sin_tab = cos_ref[0], sin_ref[0]
    for g in range(k_ref.shape[1]):
        o_ref[0, g] = rope_block(k_ref[0, g], cos_tab, sin_tab)


def k_rope(k_proj, cos_tab, sin_tab):
    nb, n_kv, tok, hd = k_proj.shape
    tab = pl.BlockSpec((1, tok, hd), lambda b: (b, 0, 0))
    blk = pl.BlockSpec((1, n_kv, tok, hd), lambda b: (b, 0, 0, 0))
    return pl.pallas_call(
        k_rope_kernel,
        grid=(nb,),
        in_specs=[blk, tab, tab],
        out_specs=blk,
        out_shape=jax.ShapeDtypeStruct(k_proj.shape, jnp.bfloat16),
        cost_estimate=pl.CostEstimate(flops=nb * n_kv * tok * hd * 400, bytes_accessed=nb * n_kv * tok * hd * 4, transcendentals=0),
    )(k_proj, cos_tab, sin_tab)


def attn_kernel(n_ref, q_ref, k_ref, v_ref, cos_ref, sin_ref, o_ref, qa, qb, sa, sb, pa, pb, la, lb, *, n_dev, q_per_kv):
    n_heads, tok, hd = q_ref.shape[1], q_ref.shape[2], q_ref.shape[3]
    n_pairs = n_heads // 2
    c = (hd ** -0.5) * LOG2E
    row_chunk = 64

    def rope_stage(i, q_scr):
        cos_tab, sin_tab = cos_ref[0], sin_ref[0]
        for t in range(2):
            q_scr[pl.ds(t * tok, tok), :] = rope_block(q_ref[0, 2 * i + t], cos_tab, sin_tab)

    def qk_stage(i, q_scr, s_scr, n):
        g = (2 * i) // q_per_kv
        q = q_scr[...]
        for j in range(n):
            s_scr[:, j * tok:(j + 1) * tok] = lax.dot_general(
                q, k_ref[j, 0, g], (((1,), (1,)), ((), ())), preferred_element_type=jnp.float32)

    def softmax_stage(s_scr, p_scr, l_scr, n, first_masked, me):
        for r in range(0, 2 * tok, row_chunk):
            rows = pl.ds(r, row_chunk)
            ri = lax.broadcasted_iota(jnp.int32, (row_chunk, tok), 0) + (r % tok)
            diff = lax.broadcasted_iota(jnp.int32, (row_chunk, tok), 1) - ri

            def scores(j):
                val = s_scr[rows, j * tok:(j + 1) * tok]
                if j < first_masked:
                    return val
                limit = 0 if first_masked == n - 1 else (me - j) * tok
                return jnp.where(diff <= limit, val, -jnp.inf)

            mx = scores(0)
            for j in range(1, n):
                mx = jnp.maximum(mx, scores(j))
            mx = jnp.max(mx, axis=1, keepdims=True)
            tot = None
            for j in range(n):
                pj = jnp.exp2((scores(j) - mx) * c)
                p_scr[rows, j * tok:(j + 1) * tok] = pj.astype(jnp.bfloat16)
                part = pj[:, :hd] + pj[:, hd:]
                tot = part if tot is None else tot + part
            l_scr[rows, :] = jnp.broadcast_to(jnp.sum(tot, axis=1, keepdims=True), (row_chunk, hd))

    def pv_stage(i, p_scr, l_scr, n):
        g = (2 * i) // q_per_kv
        acc = None
        for j in range(n):
            part = jnp.dot(p_scr[:, j * tok:(j + 1) * tok], v_ref[j, 0, g], preferred_element_type=jnp.float32)
            acc = part if acc is None else acc + part
        out = (acc / l_scr[...]).astype(jnp.bfloat16)
        for t in range(2):
            o_ref[0, :, pl.ds(pl.multiple_of((2 * i + t) * hd, hd), hd)] = out[t * tok:(t + 1) * tok]

    def run(n, lo):
        last_pair = n_pairs - 1
        rope_stage(0, qa)
        qk_stage(0, qa, sa, n)
        rope_stage(1, qb)

        def body(it, _):
            i = 2 * it
            prev = jnp.maximum(i - 1, 0)
            qk_stage(i + 1, qb, sb, n)
            rope_stage(jnp.minimum(i + 2, last_pair), qa)
            softmax_stage(sa, pa, la, n, lo - 1, me)
            pv_stage(prev, pb, lb, n)
            qk_stage(jnp.minimum(i + 2, last_pair), qa, sa, n)
            rope_stage(jnp.minimum(i + 3, last_pair), qb)
            softmax_stage(sb, pb, lb, n, lo - 1, me)
            pv_stage(i, pa, la, n)
            return 0

        lax.fori_loop(0, n_pairs // 2, body, 0)
        pv_stage(last_pair, pb, lb, n)

    me = n_ref[0]
    lo = 1
    for n in VARIANTS(n_dev):
        pl.when((me + 1 >= lo) & (me < n))(functools.partial(run, n, lo))
        lo = n + 1


def attention(n_act, q, k_all, v_all, cos_tab, sin_tab):
    nb, n_heads, tok, hd = q.shape
    n_dev, _, n_kv = k_all.shape[:3]
    tab = pl.BlockSpec((1, tok, hd), lambda b, *_: (b, 0, 0))
    kv = pl.BlockSpec((n_dev, 1, n_kv, tok, hd), lambda b, *_: (0, b, 0, 0, 0))
    keys = n_dev * tok
    macs = nb * n_heads * tok * keys * hd
    return pl.pallas_call(
        functools.partial(attn_kernel, n_dev=n_dev, q_per_kv=n_heads // n_kv),
        grid_spec=pltpu.PrefetchScalarGridSpec(
            num_scalar_prefetch=1,
            grid=(nb,),
            in_specs=[pl.BlockSpec((1, n_heads, tok, hd), lambda b, *_: (b, 0, 0, 0)), kv, kv, tab, tab],
            out_specs=pl.BlockSpec((1, tok, n_heads * hd), lambda b, *_: (b, 0, 0)),
            scratch_shapes=[
                pltpu.VMEM((2 * tok, hd), jnp.bfloat16), pltpu.VMEM((2 * tok, hd), jnp.bfloat16),
                pltpu.VMEM((2 * tok, keys), jnp.float32), pltpu.VMEM((2 * tok, keys), jnp.float32),
                pltpu.VMEM((2 * tok, keys), jnp.bfloat16), pltpu.VMEM((2 * tok, keys), jnp.bfloat16),
                pltpu.VMEM((2 * tok, hd), jnp.float32), pltpu.VMEM((2 * tok, hd), jnp.float32),
            ],
        ),
        out_shape=jax.ShapeDtypeStruct((nb, tok, n_heads * hd), jnp.bfloat16),
        compiler_params=pltpu.CompilerParams(vmem_limit_bytes=60 * 1024 * 1024),
        cost_estimate=pl.CostEstimate(flops=8 * macs, bytes_accessed=2 * (2 * q.size + 2 * k_all.size), transcendentals=0),
    )(n_act, q, k_all, v_all, cos_tab, sin_tab)


def solution(mesh):
    def per_device(hidden, positions, w_q, w_k, w_v, w_o):
        n_batch, tok = hidden.shape[0], hidden.shape[1]
        n_act = lax.axis_index('cp').astype(jnp.int32).reshape(1)
        cos_tab, sin_tab = rope_tables(positions, w_q.shape[2])
        cb = n_batch // N_CHUNKS
        spans = [slice(i * cb, (i + 1) * cb) for i in range(N_CHUNKS)]

        def proj(x, w):
            return jnp.einsum('bsd,dhe->bshe', x, w, preferred_element_type=jnp.float32).astype(jnp.bfloat16).transpose(0, 2, 1, 3)

        k_all, v_all = [], []
        for sp in spans:
            kr = k_rope(proj(hidden[sp], w_k), cos_tab[sp], sin_tab[sp])
            k_all.append(lax.all_gather(kr, 'cp'))
            v_all.append(lax.all_gather(with_layout_constraint(proj(hidden[sp], w_v), Layout((0, 1, 2, 3))), 'cp'))
        w_o2 = w_o.reshape(-1, w_o.shape[2])
        outs = []
        for i, sp in enumerate(spans):
            q = proj(hidden[sp], w_q)
            attn = attention(n_act, q, k_all[i], v_all[i], cos_tab[sp], sin_tab[sp])
            y = jnp.einsum('bsf,fd->bsd', attn, w_o2, preferred_element_type=jnp.float32)
            outs.append((hidden[sp].astype(jnp.float32) + y).astype(jnp.bfloat16))
        return jnp.concatenate(outs, axis=0)

    rep = P(None, None, None)
    return jax.shard_map(per_device, mesh=mesh, in_specs=(P('dp', 'cp', None), P('dp', 'cp'), rep, rep, rep, rep), out_specs=P('dp', 'cp', None), check_vma=False)
```

time: 3090 us -> 1060 us (0.34)
  the two profiles are of different devices: /device:TPU:112 before, /device:TPU:119 now
where the time goes in v1:
time: 1060 us
  matrix products  508 us (48%)
  Pallas kernels  480 us (45%)
  other arithmetic  37.6 us (4%)
  waiting for transfers between devices  14.4 us (1%)
  between operations  13.4 us (1%)
    pallas_call x2, Pallas kernels, attention(): pl.pallas_call(functools.partial(attn_kernel, n_dev=n_dev, q_per_kv=n_hea...  464 us
    dot_general x6, matrix products, proj(): jnp.einsum('bsd,dhe->bshe', x, w, preferred_element_type=jnp.float32)  315 us
    dot_general x2, matrix products, per_device(): jnp.einsum('bsf,fd->bsd', attn, w_o2, preferred_element_type=jnp.float32)  194 us
    concatenate x1, other arithmetic, per_device(): return jnp.concatenate(outs, axis=0)  28.5 us
  transfers between devices with their start and end apart: 4, of which 1 were waited for; matrix products, arithmetic and copies ran while one was open for 36% of the time, Pallas kernels for 23%

profile of v1, /device:TPU:119, one launch (start us, length us, event | category | flops | bytes accessed | tf_op | source)
XLA Modules:
  0.0 1056.7 jit_solution(11316802208431630545)
XLA Ops:
  6.5 0.0 all-gather.9.cloned.1.call-start
  6.6 0.7 convert_element_type.62
  7.3 0.6 broadcast_multiply_fusion
  7.9 7.8 sine_multiply_fusion
  15.7 2.0 fusion.53
  17.7 28.8 %convert_bitcast_fusion.5.k_ref = bf16[8,8,256,128]{3,2,1,0:T(8,128)(2,1)} fusion(bf16[5120,8,128]{2,1,0:T(8,128)(2,1)} %param.9, bf16[16,256,5120]{2,1,0:T(8,128)(2,1)} %param.6), kind=kOutput, calls=%fused_computation.36 | convolution fusion | flops 21476933632 | bytes 35651584 | tf_op jit(solution)/shard_map/bsd,dhe->bshe/dot_general | solution.py:172
  46.6 7.8 shard_map.64
  54.4 0.1 all-gather.9.cloned.1.call-update
  54.5 0.4 all-gather.11.cloned.1.call-start
  54.8 29.0 %convert_bitcast_fusion.4 = bf16[8,8,256,128]{3,2,1,0:T(8,128)(2,1)} fusion(bf16[5120,8,128]{2,1,0:T(8,128)(2,1)} %param.10, bf16[16,256,5120]{2,1,0:T(8,128)(2,1)} %param.6), kind=kOutput, calls=%fused_computation.35 | convolution fusion | flops 21476933632 | bytes 35651584 | tf_op jit(solution)/shard_map/bsd,dhe->bshe/dot_general | solution.py:172
  83.8 0.1 all-gather.11.cloned.1.call-update
  83.9 0.1 all-gather.13.cloned.1.call-start
  84.0 28.9 %convert_bitcast_fusion.3.k_ref = bf16[8,8,256,128]{3,2,1,0:T(8,128)(2,1)} fusion(bf16[5120,8,128]{2,1,0:T(8,128)(2,1)} %param.9, bf16[16,256,5120]{2,1,0:T(8,128)(2,1)} %param.6), kind=kOutput, calls=%fused_computation.34 | convolution fusion | flops 21476933632 | bytes 35651584 | tf_op jit(solution)/shard_map/bsd,dhe->bshe/dot_general | solution.py:172
  112.8 7.8 shard_map.66
  120.7 0.1 all-gather.13.cloned.1.call-update
  120.7 0.6 all-gather.15.cloned.1.call-start
  121.3 29.0 %convert_bitcast_fusion.2 = bf16[8,8,256,128]{3,2,1,0:T(8,128)(2,1)} fusion(bf16[5120,8,128]{2,1,0:T(8,128)(2,1)} %param.10, bf16[16,256,5120]{2,1,0:T(8,128)(2,1)} %param.6), kind=kOutput, calls=%fused_computation.33 | convolution fusion | flops 21476933632 | bytes 35651584 | tf_op jit(solution)/shard_map/bsd,dhe->bshe/dot_general | solution.py:172
  150.3 0.1 all-gather.15.cloned.1.call-update
  150.4 99.3 %convert_bitcast_fusion.1.q_ref = bf16[8,32,256,128]{3,2,1,0:T(8,128)(2,1)} fusion(bf16[5120,32,128,1]{2,1,0,3:T(8,128)(2,1)} %bitcast.81, bf16[16,256,5120]{2,1,0:T(8,128)(2,1)} %param.6), kind=kOutput, calls=%fused_computation.18 | convolution fusion | flops 85907734528 | bytes 79691776 | tf_op jit(solution)/shard_map/bsd,dhe->bshe/dot_general | solution.py:172
  249.7 99.6 %convert_bitcast_fusion.q_ref = bf16[8,32,256,128]{3,2,1,0:T(8,128)(2,1)} fusion(bf16[5120,32,128,1]{2,1,0,3:T(8,128)(2,1)} %bitcast.82, bf16[16,256,5120]{2,1,0:T(8,128)(2,1)} %param.6), kind=kOutput, calls=%fused_computation.17 | convolution fusion | flops 85907734528 | bytes 79691776 | tf_op jit(solution)/shard_map/bsd,dhe->bshe/dot_general | solution.py:172
  349.2 0.0 all-gather.9.cloned.1.call-done
  349.2 14.2 %all-gather.11.cloned.1.call-done = bf16[64,8,256,128]{3,2,1,0:T(8,128)(2,1)} async-done(((bf16[8,8,256,128]{3,2,1,0:T(8,128)(2,1)}), bf16[64,8,256,128]{3,2,1,0:T(8,128)(2,1)}) %all-gather.11.cloned.1.call-update) | async-done | bytes 33554448 | tf_op jit(solution)/shard_map/all_gather | solution.py:178
  363.4 232.1 %shard_map.65 = bf16[8,256,4096]{2,1,0:T(8,128)(2,1)} custom-call(s32[1]{0:T(128)} %bitcast.n_ref, bf16[8,32,256,128]{3,2,1,0:T(8,128)(2,1)} %convert_bitcast_fusion.1.q_ref, bf16[8,8,8,256,128]{4,3,2,1,0:T(8,128)(2,1)} %bitcast.85, bf16[8,8,8,256,128]{4,3,2,1,0:T(8,128)(2,1)} %bitcast.87, f32[8,256,128]{2,1,0:T(8,128)} %get-tuple-element.12.cos_ref, ...), custom_call_target="tpu_custom_call" | custom-call | flops 137438953472 | bytes 100663296 | tf_op jit(solution)/shard_map/pallas_call | solution.py:143
  595.5 97.1 %add_convert_fusion.1 = bf16[8,256,5120]{2,1,0:T(8,128)(2,1)} fusion(bf16[8,256,4096]{2,1,0:T(8,128)(2,1)} %shard_map.65, bf16[4096,5120,1]{1,0,2:T(8,128)(2,1)} %bitcast.83, bf16[16,256,5120]{2,1,0:T(8,128)(2,1)} %param.6), kind=kOutput, calls=%fused_computation.2 | convolution fusion | flops 85930803200 | bytes 100663296 | tf_op jit(solution)/shard_map/bsf,fd->bsd/dot_general | solution.py:184
  692.6 0.0 all-gather.13.cloned.1.call-done
  692.6 0.0 all-gather.15.cloned.1.call-done
  692.6 232.1 %shard_map.67 = bf16[8,256,4096]{2,1,0:T(8,128)(2,1)} custom-call(s32[1]{0:T(128)} %bitcast.n_ref, bf16[8,32,256,128]{3,2,1,0:T(8,128)(2,1)} %convert_bitcast_fusion.q_ref, bf16[8,8,8,256,128]{4,3,2,1,0:T(8,128)(2,1)} %bitcast.86, bf16[8,8,8,256,128]{4,3,2,1,0:T(8,128)(2,1)} %bitcast.88, f32[8,256,128]{2,1,0:T(8,128)} %get-tuple-element.11.cos_ref, ...), custom_call_target="tpu_custom_call" | custom-call | flops 137438953472 | bytes 100663296 | tf_op jit(solution)/shard_map/pallas_call | solution.py:143
  924.6 96.8 %add_convert_fusion = bf16[8,256,5120]{2,1,0:T(8,128)(2,1)} fusion(bf16[8,256,4096]{2,1,0:T(8,128)(2,1)} %shard_map.67, bf16[4096,5120,1]{1,0,2:T(8,128)(2,1)} %bitcast.84, bf16[16,256,5120]{2,1,0:T(8,128)(2,1)} %param.6), kind=kOutput, calls=%fused_computation.1 | convolution fusion | flops 85930803200 | bytes 100663296 | tf_op jit(solution)/shard_map/bsf,fd->bsd/dot_general | solution.py:184
  1021.5 28.5 %pad_maximum_fusion = bf16[16,256,5120]{2,1,0:T(8,128)(2,1)} fusion(bf16[8,256,5120]{2,1,0:T(8,128)(2,1)} %add_convert_fusion, bf16[8,256,5120]{2,1,0:T(8,128)(2,1)} %add_convert_fusion.1), kind=kLoop, calls=%fused_computation | loop fusion | flops 20971520 | bytes 83886080 | tf_op jit(solution)/shard_map/concatenate | solution.py:186
  (2 shorter events, 0.0 us)
Async XLA Ops:
  6.5 342.7 %all-gather.9.cloned.1.call-start = ((), (), s32[]{:S(2)}) async-start(), calls=%async_computation | async-start | bytes 37748736 | tf_op jit(solution)/shard_map/all_gather | solution.py:177
  54.5 308.9 %all-gather.11.cloned.1.call-start = ((), (), s32[]{:S(2)}) async-start(), calls=%async_computation.1 | async-start | bytes 37748736 | tf_op jit(solution)/shard_map/all_gather | solution.py:178
  83.9 608.7 %all-gather.13.cloned.1.call-start = ((), (), s32[]{:S(2)}) async-start(), calls=%async_computation.2 | async-start | bytes 37748736 | tf_op jit(solution)/shard_map/all_gather | solution.py:177
  120.7 571.8 %all-gather.15.cloned.1.call-start = ((), (), s32[]{:S(2)}) async-start(), calls=%async_computation.3 | async-start | bytes 37748736 | tf_op jit(solution)/shard_map/all_gather | solution.py:178
Sparse Core Ops, SparseCore 0:
  54.6 153.5 all-gather.8
  209.8 153.5 all-gather.10
  365.0 153.5 all-gather.12
  520.1 153.5 all-gather.14

commit v2 on v1

v2 whole, which is shorter than its diff:
```python
import functools

import jax
import jax.numpy as jnp
from jax import lax
from jax.experimental import pallas as pl
from jax.experimental.pallas import tpu as pltpu
from jax.experimental.layout import Layout, with_layout_constraint
from jax.sharding import PartitionSpec as P

ROPE_BASE = 500000.0
LOG2E = 1.4426950408889634
CHUNK_PARTS = (3, 3, 2)


def VARIANTS(n_dev):
    return sorted({max(n_dev // 2 - 1, 1), max(n_dev - 1, 1), n_dev})


def rope_tables(positions, head_dim):
    half = head_dim // 2
    inv_freq = ROPE_BASE ** (-jnp.arange(0, head_dim, 2, dtype=jnp.float32) / head_dim)
    angles = positions.astype(jnp.float32)[..., None] * inv_freq
    angles = jnp.concatenate([angles, angles], axis=-1)
    sign = jnp.where(jnp.arange(head_dim) < half, -1.0, 1.0).astype(jnp.float32)
    return jnp.cos(angles), jnp.sin(angles) * sign


def rope_block(val, cos_tab, sin_tab):
    v = val.astype(jnp.float32)
    return (v * cos_tab + pltpu.roll(v, v.shape[-1] // 2, v.ndim - 1) * sin_tab).astype(jnp.bfloat16)


def k_rope_kernel(k_ref, cos_ref, sin_ref, o_ref):
    for b in range(k_ref.shape[0]):
        cos_tab, sin_tab = cos_ref[b], sin_ref[b]
        for g in range(k_ref.shape[1]):
            o_ref[b, g] = rope_block(k_ref[b, g], cos_tab, sin_tab)


def k_rope(k_proj, cos_tab, sin_tab):
    nb, n_kv, tok, hd = k_proj.shape
    bb = 2 if nb % 2 == 0 else 1
    tab = pl.BlockSpec((bb, tok, hd), lambda b: (b, 0, 0))
    blk = pl.BlockSpec((bb, n_kv, tok, hd), lambda b: (b, 0, 0, 0))
    return pl.pallas_call(
        k_rope_kernel,
        grid=(nb // bb,),
        in_specs=[blk, tab, tab],
        out_specs=blk,
        out_shape=jax.ShapeDtypeStruct(k_proj.shape, jnp.bfloat16),
        cost_estimate=pl.CostEstimate(flops=nb * n_kv * tok * hd * 400, bytes_accessed=nb * n_kv * tok * hd * 4, transcendentals=0),
    )(k_proj, cos_tab, sin_tab)


def attn_kernel(n_ref, q_ref, k_ref, v_ref, cos_ref, sin_ref, o_ref, qa, qb, sa, sb, pa, pb, la, lb, vt, *, n_dev, q_per_kv):
    n_heads, tok, hd = q_ref.shape[1], q_ref.shape[2], q_ref.shape[3]
    n_pairs = n_heads // 2
    c = (hd ** -0.5) * LOG2E
    row_chunk = 32
    assert q_per_kv == 4

    def rope_stage(i, q_scr):
        cos_tab, sin_tab = cos_ref[0], sin_ref[0]
        for t in range(2):
            q_scr[pl.ds(t * tok, tok), :] = rope_block(q_ref[0, 2 * i + t], cos_tab, sin_tab)

    def vt_stage(i, n):
        g = (2 * i) // q_per_kv
        for j in range(n):
            vt[:, j * tok:(j + 1) * tok] = v_ref[j, 0, g].T

    def qk_stage(i, q_scr, s_scr, n):
        g = (2 * i) // q_per_kv
        s_scr[:n * tok, :] = lax.dot_general(
            k_ref[:n, 0, g].reshape(n * tok, hd), q_scr[...], (((1,), (1,)), ((), ())), preferred_element_type=jnp.float32)

    def softmax_stage(s_scr, p_scr, l_scr, n, first_masked, me):
        for t in range(2):
            cols = slice(t * tok, (t + 1) * tok)
            diff = lax.broadcasted_iota(jnp.int32, (row_chunk, tok), 0) - lax.broadcasted_iota(jnp.int32, (row_chunk, tok), 1)

            def scores(r):
                val = s_scr[r:r + row_chunk, cols]
                j = r // tok
                if j < first_masked:
                    return val
                limit = -(r % tok) if first_masked == n - 1 else me * tok - r
                return jnp.where(diff <= limit, val, -jnp.inf)

            mx = scores(0)
            for r in range(row_chunk, n * tok, row_chunk):
                mx = jnp.maximum(mx, scores(r))
            mx = jnp.max(mx, axis=0, keepdims=True)
            tot = None
            for r in range(0, n * tok, row_chunk):
                pj = jnp.exp2((scores(r) - mx) * c)
                p_scr[r:r + row_chunk, cols] = pj.astype(jnp.bfloat16)
                tot = pj if tot is None else tot + pj
            l_scr[:, cols] = jnp.broadcast_to(jnp.sum(tot, axis=0, keepdims=True), (8, tok))

    def pv_stage(i, p_scr, l_scr, n):
        acc = jnp.dot(vt[:, :n * tok], p_scr[:n * tok, :], preferred_element_type=jnp.float32)
        out = acc * (1.0 / l_scr[0:1, :])
        for t in range(2):
            o_ref[0, :, pl.ds(pl.multiple_of((2 * i + t) * hd, hd), hd)] = out[:, t * tok:(t + 1) * tok].T.astype(jnp.bfloat16)

    def run(n, lo):
        last_pair = n_pairs - 1
        rope_stage(0, qa)
        qk_stage(0, qa, sa, n)
        rope_stage(1, qb)

        def body(it, _):
            i = 2 * it
            prev = jnp.maximum(i - 1, 0)
            qk_stage(i + 1, qb, sb, n)
            rope_stage(jnp.minimum(i + 2, last_pair), qa)
            softmax_stage(sa, pa, la, n, lo - 1, me)
            pv_stage(prev, pb, lb, n)
            vt_stage(i, n)
            qk_stage(jnp.minimum(i + 2, last_pair), qa, sa, n)
            rope_stage(jnp.minimum(i + 3, last_pair), qb)
            softmax_stage(sb, pb, lb, n, lo - 1, me)
            pv_stage(i, pa, la, n)
            return 0

        lax.fori_loop(0, n_pairs // 2, body, 0)
        pv_stage(last_pair, pb, lb, n)

    me = n_ref[0]
    lo = 1
    for n in VARIANTS(n_dev):
        pl.when((me + 1 >= lo) & (me < n))(functools.partial(run, n, lo))
        lo = n + 1


def attention(n_act, q, k_all, v_all, cos_tab, sin_tab):
    nb, n_heads, tok, hd = q.shape
    n_dev, _, n_kv = k_all.shape[:3]
    tab = pl.BlockSpec((1, tok, hd), lambda b, *_: (b, 0, 0))
    kv = pl.BlockSpec((n_dev, 1, n_kv, tok, hd), lambda b, *_: (0, b, 0, 0, 0))
    keys = n_dev * tok
    macs = nb * n_heads * tok * keys * hd
    return pl.pallas_call(
        functools.partial(attn_kernel, n_dev=n_dev, q_per_kv=n_heads // n_kv),
        grid_spec=pltpu.PrefetchScalarGridSpec(
            num_scalar_prefetch=1,
            grid=(nb,),
            in_specs=[pl.BlockSpec((1, n_heads, tok, hd), lambda b, *_: (b, 0, 0, 0)), kv, kv, tab, tab],
            out_specs=pl.BlockSpec((1, tok, n_heads * hd), lambda b, *_: (b, 0, 0)),
            scratch_shapes=[
                pltpu.VMEM((2 * tok, hd), jnp.bfloat16), pltpu.VMEM((2 * tok, hd), jnp.bfloat16),
                pltpu.VMEM((keys, 2 * tok), jnp.float32), pltpu.VMEM((keys, 2 * tok), jnp.float32),
                pltpu.VMEM((keys, 2 * tok), jnp.bfloat16), pltpu.VMEM((keys, 2 * tok), jnp.bfloat16),
                pltpu.VMEM((8, 2 * tok), jnp.float32), pltpu.VMEM((8, 2 * tok), jnp.float32),
                pltpu.VMEM((hd, keys), jnp.bfloat16),
            ],
        ),
        out_shape=jax.ShapeDtypeStruct((nb, tok, n_heads * hd), jnp.bfloat16),
        compiler_params=pltpu.CompilerParams(vmem_limit_bytes=60 * 1024 * 1024),
        cost_estimate=pl.CostEstimate(flops=8 * macs, bytes_accessed=2 * (2 * q.size + 2 * k_all.size), transcendentals=0),
    )(n_act, q, k_all, v_all, cos_tab, sin_tab)


def blank(shape, dtype):
    return pl.pallas_call(lambda o_ref: None, out_specs=pl.BlockSpec(memory_space=pl.ANY), out_shape=jax.ShapeDtypeStruct(shape, dtype))()


def solution(mesh):
    def per_device(hidden, positions, w_q, w_k, w_v, w_o):
        n_batch, tok = hidden.shape[0], hidden.shape[1]
        n_act = lax.axis_index('cp').astype(jnp.int32).reshape(1)
        cos_tab, sin_tab = rope_tables(positions, w_q.shape[2])
        unit = n_batch // sum(CHUNK_PARTS)
        ends = [unit * sum(CHUNK_PARTS[:i + 1]) for i in range(len(CHUNK_PARTS))]
        spans = [slice(e - unit * p, e) for e, p in zip(ends, CHUNK_PARTS)]

        def proj(x, w):
            return jnp.einsum('bsd,dhe->bshe', x, w, preferred_element_type=jnp.float32).astype(jnp.bfloat16).transpose(0, 2, 1, 3)

        k_all, v_all = [], []
        for sp in spans:
            kr = k_rope(proj(hidden[sp], w_k), cos_tab[sp], sin_tab[sp])
            k_all.append(lax.all_gather(kr, 'cp'))
            v_all.append(lax.all_gather(with_layout_constraint(proj(hidden[sp], w_v), Layout((0, 1, 2, 3))), 'cp'))
        w_o2 = w_o.reshape(-1, w_o.shape[2])
        out = blank(hidden.shape, hidden.dtype)
        for i, sp in enumerate(spans):
            q = proj(hidden[sp], w_q)
            attn = attention(n_act, q, k_all[i], v_all[i], cos_tab[sp], sin_tab[sp])
            y = jnp.einsum('bsf,fd->bsd', attn, w_o2, preferred_element_type=jnp.float32)
            y = (hidden[sp].astype(jnp.float32) + y).astype(jnp.bfloat16)
            out = lax.dynamic_update_slice(out, y, (sp.start, 0, 0))
        return out

    rep = P(None, None, None)
    return jax.shard_map(per_device, mesh=mesh, in_specs=(P('dp', 'cp', None), P('dp', 'cp'), rep, rep, rep, rep), out_specs=P('dp', 'cp', None), check_vma=False)
```

time: 1060 us -> 980 us (0.925)
  the two profiles are of different devices: /device:TPU:119 before, /device:TPU:115 now
where the time goes in v2:
time: 980 us; the launch traced here: 974 us
  matrix products  528 us (54%)
  Pallas kernels  416 us (42%)
  between operations  14 us (1%)
    pallas_call x3, Pallas kernels, attention(): pl.pallas_call(functools.partial(attn_kernel, n_dev=n_dev, q_per_kv=n_hea...  402 us
    dot_general x9, matrix products, proj(): jnp.einsum('bsd,dhe->bshe', x, w, preferred_element_type=jnp.float32)  328 us
    dot_general x3, matrix products, per_device(): jnp.einsum('bsf,fd->bsd', attn, w_o2, preferred_element_type=jnp.float32)  199 us
  transfers between devices with their start and end apart: 6, of which 0 were waited for; matrix products, arithmetic and copies ran while one was open for 40% of the time, Pallas kernels for 27%

profile of v2, /device:TPU:115, one launch (start us, length us, event | category | flops | bytes accessed | tf_op | source)
XLA Modules:
  0.0 974.3 jit_solution(9660976517225691052)
XLA Ops:
  6.5 0.0 all-gather.21.cloned.1.call-start
  6.6 0.7 convert_element_type.89
  7.3 0.6 broadcast_multiply_fusion
  7.9 7.8 sine_multiply_fusion
  15.7 0.0 copy-start
  15.7 1.3 copy-done
  17.0 0.8 slice.55.cos_ref
  17.9 0.9 slice.56.sin_ref
  18.7 17.7 %convert_bitcast_fusion.8.k_ref = bf16[4,8,256,128]{3,2,1,0:T(8,128)(2,1)} fusion(bf16[5120,8,128]{2,1,0:T(8,128)(2,1)} %param.9, bf16[16,256,5120]{2,1,0:T(8,128)(2,1)} %param.6), kind=kOutput, calls=%fused_computation.57 | convolution fusion | flops 10738466816 | bytes 23068672 | tf_op jit(solution)/shard_map/bsd,dhe->bshe/dot_general | solution.py:180
  36.4 3.3 shard_map.69
  39.7 0.1 all-gather.21.cloned.1.call-update
  39.7 0.3 all-gather.23.cloned.1.call-start
  40.0 17.7 %convert_bitcast_fusion.7 = bf16[4,8,256,128]{3,2,1,0:T(8,128)(2,1)} fusion(bf16[5120,8,128]{2,1,0:T(8,128)(2,1)} %param.10, bf16[16,256,5120]{2,1,0:T(8,128)(2,1)} %param.6), kind=kOutput, calls=%fused_computation.56 | convolution fusion | flops 10738466816 | bytes 23068672 | tf_op jit(solution)/shard_map/bsd,dhe->bshe/dot_general | solution.py:180
  57.7 0.1 all-gather.23.cloned.1.call-update
  57.8 0.1 all-gather.13.cloned.1.call-start
  57.9 3.1 fusion.82
  60.9 23.0 %convert_bitcast_fusion.6.k_ref = bf16[6,8,256,128]{3,2,1,0:T(8,128)(2,1)} fusion(bf16[5120,8,128]{2,1,0:T(8,128)(2,1)} %param.9, bf16[16,256,5120]{2,1,0:T(8,128)(2,1)} %param.6), kind=kOutput, calls=%fused_computation.54 | convolution fusion | flops 16107700224 | bytes 29360128 | tf_op jit(solution)/shard_map/bsd,dhe->bshe/dot_general | solution.py:180
  83.9 5.4 shard_map.65
  89.3 0.1 all-gather.13.cloned.1.call-update
  89.4 0.1 all-gather.15.cloned.1.call-start
  89.5 23.1 %convert_bitcast_fusion.5 = bf16[6,8,256,128]{3,2,1,0:T(8,128)(2,1)} fusion(bf16[5120,8,128]{2,1,0:T(8,128)(2,1)} %param.10, bf16[16,256,5120]{2,1,0:T(8,128)(2,1)} %param.6), kind=kOutput, calls=%fused_computation.53 | convolution fusion | flops 16107700224 | bytes 29360128 | tf_op jit(solution)/shard_map/bsd,dhe->bshe/dot_general | solution.py:180
  112.6 0.1 all-gather.15.cloned.1.call-update
  112.7 0.5 all-gather.17.cloned.1.call-start
  113.1 23.0 %convert_bitcast_fusion.4.k_ref = bf16[6,8,256,128]{3,2,1,0:T(8,128)(2,1)} fusion(bf16[5120,8,128]{2,1,0:T(8,128)(2,1)} %param.9, bf16[16,256,5120]{2,1,0:T(8,128)(2,1)} %param.6), kind=kOutput, calls=%fused_computation.52 | convolution fusion | flops 16107700224 | bytes 29360128 | tf_op jit(solution)/shard_map/bsd,dhe->bshe/dot_general | solution.py:180
  136.1 5.3 shard_map.67
  141.5 0.1 all-gather.17.cloned.1.call-update
  141.5 0.1 all-gather.19.cloned.1.call-start
  141.6 23.0 %convert_bitcast_fusion.3 = bf16[6,8,256,128]{3,2,1,0:T(8,128)(2,1)} fusion(bf16[5120,8,128]{2,1,0:T(8,128)(2,1)} %param.10, bf16[16,256,5120]{2,1,0:T(8,128)(2,1)} %param.6), kind=kOutput, calls=%fused_computation.51 | convolution fusion | flops 16107700224 | bytes 29360128 | tf_op jit(solution)/shard_map/bsd,dhe->bshe/dot_general | solution.py:180
  164.6 0.1 all-gather.19.cloned.1.call-update
  164.7 74.1 %convert_bitcast_fusion.1.q_ref = bf16[6,32,256,128]{3,2,1,0:T(8,128)(2,1)} fusion(bf16[5120,32,128,1]{2,1,0,3:T(8,128)(2,1)} %bitcast.119, bf16[16,256,5120]{2,1,0:T(8,128)(2,1)} %param.6), kind=kOutput, calls=%fused_computation.22 | convolution fusion | flops 64430800896 | bytes 70254592 | tf_op jit(solution)/shard_map/bsd,dhe->bshe/dot_general | solution.py:180
  238.8 74.3 %convert_bitcast_fusion.q_ref = bf16[6,32,256,128]{3,2,1,0:T(8,128)(2,1)} fusion(bf16[5120,32,128,1]{2,1,0,3:T(8,128)(2,1)} %bitcast.120, bf16[16,256,5120]{2,1,0:T(8,128)(2,1)} %param.6), kind=kOutput, calls=%fused_computation.21 | convolution fusion | flops 64430800896 | bytes 70254592 | tf_op jit(solution)/shard_map/bsd,dhe->bshe/dot_general | solution.py:180
  313.1 52.6 %convert_bitcast_fusion.2.q_ref = bf16[4,32,256,128]{3,2,1,0:T(8,128)(2,1)} fusion(bf16[5120,32,128,1]{2,1,0,3:T(8,128)(2,1)} %bitcast.121, bf16[16,256,5120]{2,1,0:T(8,128)(2,1)} %param.6), kind=kOutput, calls=%fused_computation.41 | convolution fusion | flops 42953867264 | bytes 60817408 | tf_op jit(solution)/shard_map/bsd,dhe->bshe/dot_general | solution.py:180
  365.7 0.0 all-gather.21.cloned.1.call-done
  365.7 0.0 all-gather.23.cloned.1.call-done
  365.7 102.0 %shard_map.70 = bf16[4,256,4096]{2,1,0:T(8,128)(2,1)} custom-call(s32[1]{0:T(128)} %bitcast.n_ref, bf16[4,32,256,128]{3,2,1,0:T(8,128)(2,1)} %convert_bitcast_fusion.2.q_ref, bf16[8,4,8,256,128]{4,3,2,1,0:T(8,128)(2,1)} %bitcast.129, bf16[8,4,8,256,128]{4,3,2,1,0:T(8,128)(2,1)} %bitcast.130, f32[4,256,128]{2,1,0:T(8,128)} %slice.55.cos_ref, ...), custom_call_target="tpu_custom_call" | custom-call | flops 68719476736 | bytes 50331648 | tf_op jit(solution)/shard_map/pallas_call | solution.py:145
  467.7 0.0 all-gather.13.cloned.1.call-done
  467.7 0.0 all-gather.15.cloned.1.call-done
  467.7 150.0 %shard_map.66 = bf16[6,256,4096]{2,1,0:T(8,128)(2,1)} custom-call(s32[1]{0:T(128)} %bitcast.n_ref, bf16[6,32,256,128]{3,2,1,0:T(8,128)(2,1)} %convert_bitcast_fusion.1.q_ref, bf16[8,6,8,256,128]{4,3,2,1,0:T(8,128)(2,1)} %bitcast.125, bf16[8,6,8,256,128]{4,3,2,1,0:T(8,128)(2,1)} %bitcast.127, f32[6,256,128]{2,1,0:T(8,128)} %get-tuple-element.11.cos_ref, ...), custom_call_target="tpu_custom_call" | custom-call | flops 103079215104 | bytes 75497472 | tf_op jit(solution)/shard_map/pallas_call | solution.py:145
  617.7 74.8 %fusion.6 = bf16[16,256,5120]{2,1,0:T(8,128)(2,1)} fusion(bf16[16,256,5120]{2,1,0:T(8,128)(2,1)} %shard_map.64, bf16[6,256,4096]{2,1,0:T(8,128)(2,1)} %shard_map.66, bf16[4096,5120,1]{1,0,2:T(8,128)(2,1)} %bitcast.122, bf16[16,256,5120]{2,1,0:T(8,128)(2,1)} %param.6), kind=kOutput, calls=%fused_computation.9 | convolution fusion | flops 64448102400 | bytes 85983232 | tf_op jit(solution)/shard_map/bsf,fd->bsd/dot_general | solution.py:192
  692.4 0.0 all-gather.17.cloned.1.call-done
  692.4 0.0 all-gather.19.cloned.1.call-done
  692.5 150.0 %shard_map.68 = bf16[6,256,4096]{2,1,0:T(8,128)(2,1)} custom-call(s32[1]{0:T(128)} %bitcast.n_ref, bf16[6,32,256,128]{3,2,1,0:T(8,128)(2,1)} %convert_bitcast_fusion.q_ref, bf16[8,6,8,256,128]{4,3,2,1,0:T(8,128)(2,1)} %bitcast.126, bf16[8,6,8,256,128]{4,3,2,1,0:T(8,128)(2,1)} %bitcast.128, f32[6,256,128]{2,1,0:T(8,128)} %get-tuple-element.12.cos_ref, ...), custom_call_target="tpu_custom_call" | custom-call | flops 103079215104 | bytes 75497472 | tf_op jit(solution)/shard_map/pallas_call | solution.py:145
  842.4 0.0 copy-start.1
  842.4 75.2 %fusion.7 = bf16[16,256,5120]{2,1,0:T(8,128)(2,1)} fusion(bf16[16,256,5120]{2,1,0:T(8,128)(2,1)} %fusion.6, bf16[6,256,4096]{2,1,0:T(8,128)(2,1)} %shard_map.68, bf16[4096,5120,1]{1,0,2:T(8,128)(2,1)} %bitcast.123, bf16[16,256,5120]{2,1,0:T(8,128)(2,1)} %param.6), kind=kOutput, calls=%fused_computation.10 | convolution fusion | flops 64448102400 | bytes 85983232 | tf_op jit(solution)/shard_map/bsf,fd->bsd/dot_general | solution.py:192
  917.6 0.0 copy-done.1
  917.6 49.4 %fusion.18 = bf16[16,256,5120]{2,1,0:T(8,128)(2,1)} fusion(bf16[16,256,5120]{2,1,0:T(8,128)(2,1)} %fusion.7, bf16[4,256,4096]{2,1,0:T(8,128)(2,1)S(1)} %copy-done.1, bf16[4096,5120,1]{1,0,2:T(8,128)(2,1)} %bitcast.124, bf16[16,256,5120]{2,1,0:T(8,128)(2,1)} %param.6), kind=kOutput, calls=%fused_computation.23 | convolution fusion | flops 42965401600 | bytes 71303168 | tf_op jit(solution)/shard_map/bsf,fd->bsd/dot_general | solution.py:192
  (3 shorter events, 0.0 us)
Async XLA Ops:
  6.5 359.1 %all-gather.21.cloned.1.call-start = ((), (), s32[]{:S(2)}) async-start(), calls=%async_computation.4 | async-start | bytes 18874368 | tf_op jit(solution)/shard_map/all_gather | solution.py:185
  15.7 1.3 copy-start
  39.7 325.9 %all-gather.23.cloned.1.call-start = ((), (), s32[]{:S(2)}) async-start(), calls=%async_computation.5 | async-start | bytes 18874368 | tf_op jit(solution)/shard_map/all_gather | solution.py:186
  57.8 409.9 %all-gather.13.cloned.1.call-start = ((), (), s32[]{:S(2)}) async-start(), calls=%async_computation | async-start | bytes 28311552 | tf_op jit(solution)/shard_map/all_gather | solution.py:185
  89.4 378.3 %all-gather.15.cloned.1.call-start = ((), (), s32[]{:S(2)}) async-start(), calls=%async_computation.1 | async-start | bytes 28311552 | tf_op jit(solution)/shard_map/all_gather | solution.py:186
  112.7 579.8 %all-gather.17.cloned.1.call-start = ((), (), s32[]{:S(2)}) async-start(), calls=%async_computation.2 | async-start | bytes 28311552 | tf_op jit(solution)/shard_map/all_gather | solution.py:185
  141.5 550.9 %all-gather.19.cloned.1.call-start = ((), (), s32[]{:S(2)}) async-start(), calls=%async_computation.3 | async-start | bytes 28311552 | tf_op jit(solution)/shard_map/all_gather | solution.py:186
  842.4 75.2 %copy-start.1 = (bf16[4,256,4096]{2,1,0:T(8,128)(2,1)S(1)}, bf16[4,256,4096]{2,1,0:T(8,128)(2,1)}, u32[]{:S(2)}) copy-start(bf16[4,256,4096]{2,1,0:T(8,128)(2,1)} %shard_map.70) | copy-start | bytes 25165828
Sparse Core Ops, SparseCore 0:
  39.9 83.0 all-gather.20
  124.5 81.6 all-gather.22
  207.8 117.5 all-gather.12
  326.8 117.5 all-gather.14
  445.9 117.5 all-gather.16
  565.0 117.5 all-gather.18
